TPU v7x, 512 devices: a 8x2x16 block of a 8x8x16 slice. The times are simulated.
512 devices in a mesh: grp: 2 (over y), hist: 16 (over z), chan: 8 (over x), seq: 2 (over core).
Axes of the slice: x: 8, y: 2, z: 16, core: 2. Of those that a mesh axis runs over, the one named last changes fastest.
The devices are a block of a 8x8x16 slice.
Arguments:
- history: bfloat16 [16, 8192, 4096], P(('grp', 'seq'), 'hist', 'chan'), parts along dimension 0, may hold values from -6 to 6
- filter_taps: bfloat16 [16384, 4096], P(('grp', 'hist'), 'chan'), parts along dimension 0, may hold values from -0.0625 to 0.0625
- skip_gain: float32 [8192], P(('grp', 'chan')), parts along dimension 0, may hold values from -4 to 4
- gate_values: bfloat16 [16, 64, 4096], P(('grp', 'seq'), 'hist', 'chan'), parts along dimension 0, may hold values from -6 to 6
Outputs:
- output: bfloat16 [16, 64, 4096], P(('grp', 'seq'), 'hist', 'chan'), parts along dimension 0
There are 2 independent parts, one for each index of `grp`. A program takes and returns all parts, laid end to end along the dimension named above; each array names one. Nothing has to cross between parts.
All inputs are finite; a program needn't handle non-finite values.
Results may differ from a plain program's by a relative error of at most 0.0085.
Values may be sent and summed in bfloat16 or wider, within the bound.
A program may use at most 64 MiB of HBM per device.

v0:
```python
import math

import jax
import jax.numpy as jnp
from jax import lax
from jax.sharding import PartitionSpec as P

NEW = 64


def from_behind(value, axis, steps):
    count = lax.axis_size(axis)
    first, last = (max(0, -steps), min(count, count - steps))
    return lax.ppermute(value, axis, [(source, source + steps) for source in range(first, last)])


def split_up(array, dim, devices):
    shape = array.shape
    pieces = array.reshape(*shape[:dim], devices, shape[dim] // devices, *shape[dim + 1 :])
    return jnp.moveaxis(pieces, dim, 0)


def sum_at_owner(array, axis, dim):
    pieces = split_up(array, dim, lax.axis_size(axis))
    arrived = lax.all_to_all(pieces, axis, split_axis=0, concat_axis=0, tiled=True)
    return arrived.sum(axis=0)


def phase_table(rows, length):
    row_ids = lax.iota(jnp.int32, rows)[:, None]
    col_ids = lax.iota(jnp.int32, length)[None, :]
    phase = row_ids * col_ids % length
    angle = 2.0 * math.pi / length * phase.astype(jnp.float32)
    return (jnp.cos(angle), jnp.sin(angle))


def split_table(table):
    upper = table.astype(jnp.bfloat16)
    lower = (table - upper.astype(jnp.float32)).astype(jnp.bfloat16)
    return (upper, lower)


def forward(data, table, form):
    upper, lower = table
    first = jnp.einsum(form, data, upper, preferred_element_type=jnp.float32)
    return first + jnp.einsum(form, data, lower, preferred_element_type=jnp.float32)


def inverse(spectra, table):
    data_upper, data_lower = split_table(spectra)
    table_upper, table_lower = table
    value = jnp.einsum("kc,ki->ic", data_upper, table_upper, preferred_element_type=jnp.float32)
    value = value + jnp.einsum(
        "kc,ki->ic", data_upper, table_lower, preferred_element_type=jnp.float32
    )
    return value + jnp.einsum(
        "kc,ki->ic", data_lower, table_upper, preferred_element_type=jnp.float32
    )


def body(history, filter_taps, skip_gain, gate_values):
    hist_count = lax.axis_size("hist")
    hist_index = lax.axis_index("hist")
    block_rows = history.shape[1]
    channels = history.shape[2]
    seq_count = history.shape[0]
    length = 2 * NEW
    groups = block_rows // NEW
    tap_rim = from_behind(filter_taps[:NEW], "hist", -1)
    extended = jnp.concatenate([filter_taps, tap_rim], axis=0)
    tap_blocks = jnp.concatenate(
        [
            extended[:block_rows].reshape(groups, NEW, channels),
            extended[NEW:].reshape(groups, NEW, channels),
        ],
        axis=1,
    )
    long_cos, long_sin = phase_table(length, length)
    short_cos, short_sin = phase_table(NEW, length)
    taps_cos = forward(tap_blocks, split_table(long_cos), "qsc,sk->qkc")
    taps_sin = forward(tap_blocks, split_table(long_sin), "qsc,sk->qkc")
    short_cos_parts = split_table(short_cos)
    short_sin_parts = split_table(short_sin)
    freq_ids = lax.iota(jnp.int32, length)[:, None]
    lag_ids = (NEW - 1 - lax.iota(jnp.int32, NEW))[None, :]
    back_angle = 2.0 * math.pi / length * (freq_ids * lag_ids % length).astype(jnp.float32)
    back_table = jnp.concatenate(
        [jnp.cos(back_angle) / length, -jnp.sin(back_angle) / length], axis=0
    )
    back_parts = split_table(back_table)
    rows_out = []
    for seq_id in range(seq_count):
        blocks_in = history[seq_id].reshape(groups, NEW, channels)
        input_cos = forward(blocks_in, short_cos_parts, "qrc,rk->qkc")
        input_sin = forward(blocks_in, short_sin_parts, "qrc,rk->qkc")
        real_part = jnp.sum(input_cos * taps_cos + input_sin * taps_sin, axis=0)
        imag_part = jnp.sum(input_sin * taps_cos - input_cos * taps_sin, axis=0)
        spectra = jnp.concatenate([real_part, imag_part], axis=0)
        rows_out.append(inverse(spectra, back_parts))
    partial_value = jnp.stack(rows_out, axis=0)
    newest_rows = history[:, block_rows - NEW :, :]
    last_flag = (hist_index == hist_count - 1).astype(jnp.float32)
    partial_value = partial_value + last_flag * skip_gain[None, None, :] * newest_rows.astype(
        jnp.float32
    )
    result = sum_at_owner(partial_value, "hist", 1)
    return (gate_values.astype(jnp.float32) * result).astype(jnp.bfloat16)


def solution(mesh):
    placed = (
        P(("grp", "seq"), "hist", "chan"),
        P(("grp", "hist"), "chan"),
        P(("grp", "chan")),
        P(("grp", "seq"), "hist", "chan"),
    )
    return jax.shard_map(
        body,
        mesh=mesh,
        in_specs=placed,
        out_specs=P(("grp", "seq"), "hist", "chan"),
        check_vma=False,
    )
```

profile of v0, /device:TPU:80, one launch (start us, length us, event | category | flops | bytes accessed | tf_op | source)
XLA Modules:
  0.0 109.0 jit_solution(15672604272545010487)
XLA Ops:
  0.0 0.8 slice.22
  0.8 1.3 %collective-permute-start = (bf16[64,512]{1,0:T(8,128)(2,1)S(1)}, bf16[64,512]{1,0:T(8,128)(2,1)S(1)}, u32[]{:S(2)}, u32[]{:S(2)}) collective-permute-start(bf16[64,512]{1,0:T(8,128)(2,1)S(1)} %slice.22), channel_id=1, source_target_pairs={{16,0},{32,16},{48,32},{64,48},{80,64},{96,80},{112,96},{128,112},... | collective-permute-start | bytes 196616 | tf_op jit(solution)/shard_map/ppermute | solution.py:14
  2.1 1.7 %fusion.192 = (bf16[1,512,512]{2,1,0:T(8,128)(2,1)S(1)}, bf16[1,512,512]{2,1,0:T(8,128)(2,1)S(1)}, bf16[1,512,512]{2,1,0:T(8,128)(2,1)S(1)}, bf16[1,512,512]{2,1,0:T(8,128)(2,1)S(1)}) fusion(bf16[4,512,512]{2,1,0:T(8,128)(2,1)} %param.4), kind=kLoop, calls=%fused_computation.213 | loop fusion | bytes 4194304 | tf_op jit(solution)/shard_map/slice | solution.py:93
  5.0 0.6 fusion.65
  6.2 0.6 fusion.67
  8.0 0.6 fusion.69
  9.2 1.9 %convolution_add_fusion.3 = f32[128,8,512]{2,0,1:T(8,128)} fusion(f32[128,8,512]{2,0,1:T(8,128)S(1)} %fusion.71, bf16[8,64,512]{2,1,0:T(8,128)(2,1)S(1)} %bitcast.112), kind=kOutput, calls=%fused_computation.11 | convolution fusion | flops 67780608 | bytes 4718592 | tf_op jit(solution)/shard_map/qrc,rk->qkc/dot_general | solution.py:46
  11.1 1.9 %convolution_add_fusion.4 = f32[128,8,512]{2,0,1:T(8,128)} fusion(f32[128,8,512]{2,0,1:T(8,128)S(1)} %fusion.65, bf16[8,64,512]{2,1,0:T(8,128)(2,1)S(1)} %bitcast.107), kind=kOutput, calls=%fused_computation.12 | convolution fusion | flops 67780608 | bytes 4718592 | tf_op jit(solution)/shard_map/qrc,rk->qkc/dot_general | solution.py:46
  13.0 1.9 %convolution_add_fusion.5 = f32[128,8,512]{2,0,1:T(8,128)} fusion(f32[128,8,512]{2,0,1:T(8,128)S(1)} %fusion.73, bf16[8,64,512]{2,1,0:T(8,128)(2,1)S(1)} %bitcast.108), kind=kOutput, calls=%fused_computation.13 | convolution fusion | flops 67780608 | bytes 4718592 | tf_op jit(solution)/shard_map/qrc,rk->qkc/dot_general | solution.py:46
  14.9 2.0 %convolution_add_fusion.6 = f32[128,8,512]{2,0,1:T(8,128)} fusion(f32[128,8,512]{2,0,1:T(8,128)S(1)} %fusion.67, bf16[8,64,512]{2,1,0:T(8,128)(2,1)S(1)} %bitcast.99), kind=kOutput, calls=%fused_computation.14 | convolution fusion | flops 67780608 | bytes 4718592 | tf_op jit(solution)/shard_map/qrc,rk->qkc/dot_general | solution.py:46
  16.9 1.9 %convolution_add_fusion.7 = f32[128,8,512]{2,0,1:T(8,128)} fusion(f32[128,8,512]{2,0,1:T(8,128)S(1)} %fusion.75, bf16[8,64,512]{2,1,0:T(8,128)(2,1)S(1)} %bitcast.100), kind=kOutput, calls=%fused_computation.15 | convolution fusion | flops 67780608 | bytes 4718592 | tf_op jit(solution)/shard_map/qrc,rk->qkc/dot_general | solution.py:46
  18.8 2.0 %convolution_add_fusion.9 = f32[128,8,512]{2,0,1:T(8,128)} fusion(f32[128,8,512]{2,0,1:T(8,128)S(1)} %fusion.77, bf16[8,64,512]{2,1,0:T(8,128)(2,1)S(1)} %bitcast.95), kind=kOutput, calls=%fused_computation.17 | convolution fusion | flops 67780608 | bytes 4718592 | tf_op jit(solution)/shard_map/qrc,rk->qkc/dot_general | solution.py:46
  20.8 1.9 %convolution_add_fusion.8 = f32[128,8,512]{2,0,1:T(8,128)} fusion(f32[128,8,512]{2,0,1:T(8,128)S(1)} %fusion.69, bf16[8,64,512]{2,1,0:T(8,128)(2,1)S(1)} %bitcast.96), kind=kOutput, calls=%fused_computation.16 | convolution fusion | flops 67780608 | bytes 4718592 | tf_op jit(solution)/shard_map/qrc,rk->qkc/dot_general | solution.py:46
  23.1 0.6 fusion.43
  23.7 0.6 fusion.41
  24.4 0.7 convolution_add_fusion.1
  25.2 0.8 copy-done.3
  26.0 0.6 copy-done.4
  26.7 0.6 copy-done.1
  27.3 0.6 copy-done.2
  27.9 4.6 %add_reduce_fusion.3 = (f32[128,512]{1,0:T(8,128)S(1)}, f32[128,512]{1,0:T(8,128)S(1)}, f32[128,512]{1,0:T(8,128)S(1)}, f32[128,512]{1,0:T(8,128)S(1)}, f32[128,...) fusion(f32[128,8,512]{2,0,1:T(8,128)} %convolution_add_fusion.8, ...), kind=kOutput, calls=%fused_computation.7 | convolution fusion | flops 153387008 | bytes 24117248 | tf_op jit(solution)/shard_map/qsc,sk->qkc/dot_general | solution.py:46
  34.6 1.0 maximum_add_fusion
  35.9 72.4 %all_to_all.5 = f32[16,4,4,512]{3,2,1,0:T(4,128)S(1)} all-to-all(f32[16,4,4,512]{3,2,1,0:T(4,128)S(1)} %bitcast.113), channel_id=1, replica_groups=mesh['grp'=2,'hist'=16,'chan'=8,'seq'=2] {'hist'}, dimensions={0} | all-to-all | bytes 1048576 | tf_op jit(solution)/shard_map/all_to_all | solution.py:25
  108.4 0.6 multiply_convert_fusion
  (41 shorter events, 6.4 us)
Async XLA Ops:
  0.8 22.1 %collective-permute-start = (bf16[64,512]{1,0:T(8,128)(2,1)S(1)}, bf16[64,512]{1,0:T(8,128)(2,1)S(1)}, u32[]{:S(2)}, u32[]{:S(2)}) collective-permute-start(bf16[64,512]{1,0:T(8,128)(2,1)S(1)} %slice.22), channel_id=1, source_target_pairs={{16,0},{32,16},{48,32},{64,48},{80,64},{96,80},{112,96},{128,112},... | collective-permute-start | bytes 196616 | tf_op jit(solution)/shard_map/ppermute | solution.py:14
  20.8 2.2 %copy-start.8 = (f32[512]{0:T(512)S(1)}, f32[512]{0:T(512)}, u32[]{:S(2)}) copy-start(f32[512]{0:T(512)} %param.6) | copy-start | bytes 6148
  20.8 2.2 %copy-start = (bf16[512,512]{1,0:T(8,128)(2,1)S(1)}, bf16[512,512]{1,0:T(8,128)(2,1)}, u32[]{:S(2)}) copy-start(bf16[512,512]{1,0:T(8,128)(2,1)} %param.5) | copy-start | bytes 1572868
  23.0 2.0 %copy-start.6 = (f32[128,8,512]{2,0,1:T(8,128)S(1)}, f32[128,8,512]{2,0,1:T(8,128)}, u32[]{:S(2)}) copy-start(f32[128,8,512]{2,0,1:T(8,128)} %convolution_add_fusion.9) | copy-start | bytes 6291460
  23.1 2.2 %copy-start.5 = (f32[128,8,512]{2,0,1:T(8,128)S(1)}, f32[128,8,512]{2,0,1:T(8,128)}, u32[]{:S(2)}) copy-start(f32[128,8,512]{2,0,1:T(8,128)} %convolution_add_fusion.7) | copy-start | bytes 6291460
  23.7 2.3 %copy-start.3 = (f32[128,8,512]{2,0,1:T(8,128)S(1)}, f32[128,8,512]{2,0,1:T(8,128)}, u32[]{:S(2)}) copy-start(f32[128,8,512]{2,0,1:T(8,128)} %convolution_add_fusion.5) | copy-start | bytes 6291460
  23.7 2.9 %copy-start.4 = (f32[128,8,512]{2,0,1:T(8,128)S(1)}, f32[128,8,512]{2,0,1:T(8,128)}, u32[]{:S(2)}) copy-start(f32[128,8,512]{2,0,1:T(8,128)} %convolution_add_fusion.6) | copy-start | bytes 6291460
  24.4 2.9 %copy-start.1 = (f32[128,8,512]{2,0,1:T(8,128)S(1)}, f32[128,8,512]{2,0,1:T(8,128)}, u32[]{:S(2)}) copy-start(f32[128,8,512]{2,0,1:T(8,128)} %convolution_add_fusion.3) | copy-start | bytes 6291460
  24.4 3.5 %copy-start.2 = (f32[128,8,512]{2,0,1:T(8,128)S(1)}, f32[128,8,512]{2,0,1:T(8,128)}, u32[]{:S(2)}) copy-start(f32[128,8,512]{2,0,1:T(8,128)} %convolution_add_fusion.4) | copy-start | bytes 6291460
  35.7 72.7 %copy-start.7 = (bf16[4,4,512]{2,1,0:T(4,128)(2,1)S(1)}, bf16[4,4,512]{2,1,0:T(4,128)(2,1)}, u32[]{:S(2)}) copy-start(bf16[4,4,512]{2,1,0:T(4,128)(2,1)} %param.7) | copy-start | bytes 49156
where the time goes:
time: 109 us
  blocking collectives  72.4 us (66%)
  matrix products  27.6 us (25%)
  local copies, waits for them, and re-layouts  5.53 us (5%)
  other arithmetic  2 us (2%)
  starting transfers between devices  1.3 us (1%)
    all_to_all x1, blocking collectives, sum_at_owner(): lax.all_to_all(pieces, axis, split_axis=0, concat_axis=0, tiled=True)  72.4 us
    dot_general x10, matrix products, forward(): jnp.einsum(form, data, lower, preferred_element_type=jnp.float32)  19.4 us
    dot_general x10, matrix products, forward(): first = jnp.einsum(form, data, upper, preferred_element_type=jnp.float32)  6.02 us
    unnamed x18, local copies, waits for them, and re-layouts  2.83 us
  transfers between devices with their start and end apart: 1, of which 0 were waited for; matrix products, arithmetic and copies ran while one was open for 19% of the time, Pallas kernels for 0%

commit v1 on v0

v1 whole, which is shorter than its diff:
```python
import functools

import jax
import jax.numpy as jnp
import numpy as np
from jax import lax
from jax.experimental import pallas as pl
from jax.experimental.pallas import tpu as pltpu
from jax.sharding import PartitionSpec as P

NEW = 64
BLOCK = 128
LENGTH = BLOCK + NEW
HALF = LENGTH // 2
MESH = pl.DeviceIdType.MESH


def tables():
    freqs = np.arange(HALF) + 0.5
    angle = 2.0 * np.pi / LENGTH * np.outer(freqs, np.arange(LENGTH))
    ahead = np.concatenate([np.cos(angle), np.sin(angle)], axis=0)
    lags = NEW - 1 - np.arange(NEW)
    angle = 2.0 * np.pi / LENGTH * np.outer(lags, freqs)
    back = np.concatenate([np.cos(angle), -np.sin(angle)], axis=1) * (2.0 / LENGTH)
    return jnp.asarray(ahead, jnp.bfloat16), jnp.asarray(back, jnp.bfloat16)


def dot(a, b):
    return jnp.dot(a, b, preferred_element_type=jnp.float32)


def kernel(
    lanes,
    history,
    filter_taps,
    skip_gain,
    ahead,
    back,
    summed,
    hist_buf,
    taps_buf,
    taps_freq,
    data_freq,
    mixed,
    send_buf,
    recv_buf,
    hist_sem,
    taps_sem,
    rim_send,
    rim_recv,
    send_sem,
    recv_sem,
):
    count = lax.axis_size("hist")
    me = lax.axis_index("hist")
    seqs, rows, channels = hist_buf.shape
    tiles = channels // lanes
    groups = rows // BLOCK

    def device(steps):
        return {"hist": lax.rem(me + steps + count, count)}

    taps_copies = [
        pltpu.make_async_copy(
            filter_taps.at[:, pl.ds(t * lanes, lanes)],
            taps_buf.at[pl.ds(0, rows), pl.ds(t * lanes, lanes)],
            taps_sem.at[t],
        )
        for t in range(tiles)
    ]
    hist_copies = [
        [
            pltpu.make_async_copy(
                history.at[b, :, pl.ds(t * lanes, lanes)],
                hist_buf.at[b, :, pl.ds(t * lanes, lanes)],
                hist_sem.at[t, b],
            )
            for b in range(seqs)
        ]
        for t in range(tiles)
    ]
    barrier = pltpu.get_barrier_semaphore()
    for k in range(1, count):
        pl.semaphore_signal(barrier, inc=1, device_id=device(k), device_id_type=MESH)
    for t in range(tiles):
        taps_copies[t].start()
        for b in range(seqs):
            hist_copies[t][b].start()

    rims = [
        pltpu.make_async_remote_copy(
            src_ref=taps_buf.at[pl.ds(0, NEW), pl.ds(t * lanes, lanes)],
            dst_ref=taps_buf.at[pl.ds(rows, NEW), pl.ds(t * lanes, lanes)],
            send_sem=rim_send.at[t],
            recv_sem=rim_recv.at[t],
            device_id=device(-1),
            device_id_type=MESH,
        )
        for t in range(tiles)
    ]
    for t in range(tiles):
        taps_copies[t].wait()
    pl.semaphore_wait(barrier, count - 1)
    for t in range(tiles):
        rims[t].start()

    sends = []
    is_last = me == count - 1
    last_flag = is_last.astype(jnp.float32)
    row_ids = lax.broadcasted_iota(jnp.int32, (NEW, lanes), 0)
    low = lax.rem(row_ids, 8) < 4
    for t in range(tiles):
        cols = pl.ds(t * lanes, lanes)
        rims[t].wait_recv()
        for g in range(groups):
            if g == groups - 1:
                rim = taps_buf[pl.ds(rows, NEW), cols]
                rim = jnp.where(is_last, jnp.zeros_like(rim), rim)
                taps = jnp.concatenate([taps_buf[pl.ds(g * BLOCK, BLOCK), cols], rim], axis=0)
            else:
                taps = taps_buf[pl.ds(g * BLOCK, LENGTH), cols]
            taps_freq[g] = dot(ahead[...], taps)
        partial = []
        for b in range(seqs):
            hist_copies[t][b].wait()
            for g in range(groups):
                data_freq[g] = dot(ahead[:, :BLOCK], hist_buf[b, pl.ds(g * BLOCK, BLOCK), cols])
            for r in range(0, HALF, 16):
                real = imag = None
                for g in range(groups):
                    tc = taps_freq[g, pl.ds(r, 16), :]
                    ts = taps_freq[g, pl.ds(HALF + r, 16), :]
                    dc = data_freq[g, pl.ds(r, 16), :]
                    ds = data_freq[g, pl.ds(HALF + r, 16), :]
                    re = tc * dc + ts * ds
                    im = tc * ds - ts * dc
                    real = re if real is None else real + re
                    imag = im if imag is None else imag + im
                mixed[pl.ds(r, 16), :] = real.astype(jnp.bfloat16)
                mixed[pl.ds(HALF + r, 16), :] = imag.astype(jnp.bfloat16)
            value = dot(back[...], mixed[...])
            newest = hist_buf[b, pl.ds(rows - NEW, NEW), cols].astype(jnp.float32)
            partial.append(value + (last_flag * skip_gain[:, cols]) * newest)
        evens, odds = [], []
        for b in range(0, seqs, 2):
            first, second = partial[b], partial[b + 1]
            evens.append(jnp.where(low, first, pltpu.roll(second, 4, 0)))
            odds.append(jnp.where(low, pltpu.roll(first, NEW - 4, 0), second))
        for d in range(count):
            source = odds if d % 2 else evens
            at = d // 2 * 8
            piece = jnp.concatenate([source[0][at : at + 8], source[1][at : at + 8]], axis=0)
            send_buf[t, d] = piece.astype(jnp.bfloat16)
        for k in range(1, count):
            owner = lax.rem(me + k, count)
            copy = pltpu.make_async_remote_copy(
                src_ref=send_buf.at[t, owner],
                dst_ref=recv_buf.at[t, k],
                send_sem=send_sem.at[t, k],
                recv_sem=recv_sem.at[t, k],
                device_id=device(k),
                device_id_type=MESH,
            )
            copy.start()
            sends.append(copy)
    for t in range(tiles):
        total = send_buf[t, me].astype(jnp.float32)
        for k in range(1, count):
            sends[t * (count - 1) + k - 1].wait_recv()
            total = total + recv_buf[t, k].astype(jnp.float32)
        summed[:, pl.ds(t * lanes, lanes)] = total
    for t in range(tiles):
        rims[t].wait_send()
    for copy in sends:
        copy.wait_send()


def body(history, filter_taps, skip_gain, gate_values):
    count = lax.axis_size("hist")
    seqs, rows, channels = history.shape
    own = gate_values.shape[1]
    lanes = min(256, channels)
    tiles = channels // lanes
    groups = rows // BLOCK
    ahead, back = tables()
    anywhere = pl.BlockSpec(memory_space=pl.ANY)
    vmem = pl.BlockSpec(memory_space=pltpu.VMEM)
    summed = pl.pallas_call(
        functools.partial(kernel, lanes),
        out_shape=jax.ShapeDtypeStruct((seqs * own, channels), jnp.float32),
        in_specs=[anywhere, anywhere, vmem, vmem, vmem],
        out_specs=vmem,
        scratch_shapes=[
            pltpu.VMEM((seqs, rows, channels), jnp.bfloat16),
            pltpu.VMEM((rows + NEW, channels), jnp.bfloat16),
            pltpu.VMEM((groups, LENGTH, lanes), jnp.float32),
            pltpu.VMEM((groups, LENGTH, lanes), jnp.float32),
            pltpu.VMEM((LENGTH, lanes), jnp.bfloat16),
            pltpu.VMEM((tiles, count, seqs * own, lanes), jnp.bfloat16),
            pltpu.VMEM((tiles, count, seqs * own, lanes), jnp.bfloat16),
            pltpu.SemaphoreType.DMA((tiles, seqs)),
            pltpu.SemaphoreType.DMA((tiles,)),
            pltpu.SemaphoreType.DMA((tiles,)),
            pltpu.SemaphoreType.DMA((tiles,)),
            pltpu.SemaphoreType.DMA((tiles, count)),
            pltpu.SemaphoreType.DMA((tiles, count)),
        ],
        compiler_params=pltpu.CompilerParams(collective_id=0, has_side_effects=True),
        name="hyena_window",
    )(history, filter_taps, skip_gain.reshape(1, channels), ahead, back)
    return (gate_values.astype(jnp.float32) * summed.reshape(seqs, own, channels)).astype(jnp.bfloat16)


def solution(mesh):
    placed = (
        P(("grp", "seq"), "hist", "chan"),
        P(("grp", "hist"), "chan"),
        P(("grp", "chan")),
        P(("grp", "seq"), "hist", "chan"),
    )
    return jax.shard_map(
        body,
        mesh=mesh,
        in_specs=placed,
        out_specs=P(("grp", "seq"), "hist", "chan"),
        check_vma=False,
    )
```

time: 109 us -> 68.6 us (0.63)
  blocking collectives: 72.4 us -> 0 us
  Pallas kernels: 0 us -> 66.9 us
  matrix products: 27.6 us -> 0 us
  local copies, waits for them, and re-layouts: 5.53 us -> 0.78 us
  other arithmetic: 2 us -> 0.62 us
  starting transfers between devices: 1.3 us -> 0 us
    all_to_all x1 -> x0, blocking collectives: 72.4 us -> none  [sum_at_owner(): lax.all_to_all(pieces, axis, split_axis=0, concat_axis=0, tiled=True)]
    pallas_call x0 -> x1, Pallas kernels: none -> 66.9 us  [body(): pl.pallas_call(functools.partial(kernel, lanes), out_shape=jax.ShapeDtype...]
    dot_general x32 -> x0, matrix products: 27.6 us -> none  [the longest x10 19.4 us: forward(): jnp.einsum(form, data, lower, preferred_element_type=jnp.float32)]
    unnamed x18 -> x2, local copies, waits for them, and re-layouts: 2.83 us -> 0.01 us
    slice x2 -> x0, local copies, waits for them, and re-layouts: 2.5 us -> none  [the longest x1 1.66 us: body(): blocks_in = history[seq_id].reshape(groups, NEW, channels)]
    ppermute x1 -> x0, starting transfers between devices: 1.3 us -> none  [from_behind(): lax.ppermute(value, axis, [(source, source + steps) for source in range(f...]
  transfers between devices with their start and end apart: 1 -> 0, of which waited for: 0 -> 0; matrix products, arithmetic and copies ran while one was open for 19% -> 0% of each run, Pallas kernels for 0% -> 0%
where the time goes in v1:
time: 68.6 us; the launch traced here: 68.3 us
  Pallas kernels  66.9 us (98%)
  local copies, waits for them, and re-layouts  0.78 us (1%)
    pallas_call x1, Pallas kernels, body(): pl.pallas_call(functools.partial(kernel, lanes), out_shape=jax.ShapeDtype...  66.9 us

profile of v1, /device:TPU:80, one launch (start us, length us, event | category | flops | bytes accessed | tf_op | source)
XLA Modules:
  0.0 68.3 jit_solution(9922832330859660120)
XLA Ops:
  0.0 0.0 copy-start
  0.0 66.9 %hyena_window.1 = f32[16,512]{1,0:T(8,128)} custom-call(bf16[4,512,512]{2,1,0:T(8,128)(2,1)} %history.1, bf16[512,512]{1,0:T(8,128)(2,1)} %filter_taps.1, f32[1,512]{1,0:T(1,128)} %bitcast.1, bf16[192,192]{1,0:T(8,128)(2,1)} %constant.4.clone.ahead, bf16[64,192]{1,0:T(8,128)(2,1)} %constant.5.clone.back), custom_call_target="tpu_custom_call" | custom-call | tf_op jit(solution)/shard_map/hyena_window/pallas_call | solution.py:188
  66.9 0.8 %reshape.7 = f32[4,4,512]{2,1,0:T(4,128)S(1)} reshape(f32[16,512]{1,0:T(8,128)} %hyena_window.1) | data formatting | bytes 65536 | tf_op jit(solution)/shard_map/reshape | solution.py:211
  67.7 0.0 copy-done
  67.7 0.6 multiply_convert_fusion
Async XLA Ops:
  0.0 67.7 %copy-start = (bf16[4,4,512]{2,1,0:T(4,128)(2,1)S(1)}, bf16[4,4,512]{2,1,0:T(4,128)(2,1)}, u32[]{:S(2)}) copy-start(bf16[4,4,512]{2,1,0:T(4,128)(2,1)} %param.9) | copy-start | bytes 49156

commit v2 on v1

v2 whole, which is shorter than its diff:
```python
import functools

import jax
import jax.numpy as jnp
import numpy as np
from jax import lax
from jax.experimental import pallas as pl
from jax.experimental.pallas import tpu as pltpu
from jax.sharding import PartitionSpec as P

NEW = 64
BLOCK = 128
LENGTH = BLOCK + NEW
HALF = LENGTH // 2
STEP = 16
MESH = pl.DeviceIdType.MESH


def tables():
    freqs = np.arange(HALF) + 0.5
    angle = 2.0 * np.pi / LENGTH * np.outer(freqs, np.arange(LENGTH))
    ahead = np.concatenate([np.cos(angle), np.sin(angle)], axis=0)
    lags = NEW - 1 - np.arange(NEW)
    angle = 2.0 * np.pi / LENGTH * np.outer(lags, freqs)
    back = np.concatenate([np.cos(angle), -np.sin(angle)], axis=1) * (2.0 / LENGTH)
    return jnp.asarray(ahead, jnp.bfloat16), jnp.asarray(back, jnp.bfloat16)


def dot(a, b):
    return jnp.dot(a, b, preferred_element_type=jnp.float32)


def kernel(
    lanes,
    history,
    filter_taps,
    skip_gain,
    gate_values,
    ahead_table,
    back_table,
    output,
    hist_buf,
    taps_buf,
    skip_buf,
    gate_buf,
    ahead,
    back,
    taps_freq,
    data_freq,
    last_freq,
    mixed,
    partial,
    send_buf,
    recv_buf,
    hist_sem,
    taps_sem,
    head_sem,
    small_sem,
    rim_send,
    rim_recv,
    send_sem,
    recv_sem,
    ready_sem,
):
    count = lax.axis_size("hist")
    me = lax.axis_index("hist")
    seqs, rows, channels = hist_buf.shape
    own = NEW // count
    tiles = channels // lanes
    groups = rows // BLOCK
    last = count - 1

    late = max(count - 3, 1)
    order = list(range(1, late)) + [0] + list(range(late, count))
    place = jnp.where(me == 0, late - 1, jnp.where(me < late, me - 1, me))

    def cols(t):
        return pl.ds(t * lanes, lanes)

    heads = [
        pltpu.make_async_copy(
            filter_taps.at[pl.ds(0, NEW), cols(t)],
            taps_buf.at[pl.ds(0, NEW), cols(t)],
            head_sem.at[t],
        )
        for t in range(tiles)
    ]
    taps_copies = [
        pltpu.make_async_copy(
            filter_taps.at[pl.ds(NEW, rows - NEW), cols(t)],
            taps_buf.at[pl.ds(NEW, rows - NEW), cols(t)],
            taps_sem.at[t],
        )
        for t in range(tiles)
    ]
    hist_copies = [
        [
            pltpu.make_async_copy(
                history.at[b, :, cols(t)], hist_buf.at[b, :, cols(t)], hist_sem.at[t, b]
            )
            for b in range(seqs)
        ]
        for t in range(tiles)
    ]
    smalls = [
        pltpu.make_async_copy(source, target, small_sem.at[i])
        for i, (source, target) in enumerate(
            [
                (ahead_table, ahead),
                (back_table, back),
                (skip_gain, skip_buf),
                (gate_values, gate_buf),
            ]
        )
    ]
    for copy in heads:
        copy.start()
    smalls[0].start()
    for t in range(tiles):
        taps_copies[t].start()
        for b in range(seqs):
            hist_copies[t][b].start()
    for copy in smalls[1:]:
        copy.start()

    barrier = pltpu.get_barrier_semaphore()
    for spot, other in enumerate(order):

        @pl.when(place < spot)
        def _():
            pl.semaphore_signal(barrier, inc=1, device_id={"hist": other}, device_id_type=MESH)

    def rim(t):
        return pltpu.make_async_remote_copy(
            src_ref=taps_buf.at[pl.ds(0, NEW), cols(t)],
            dst_ref=taps_buf.at[pl.ds(rows, NEW), cols(t)],
            send_sem=rim_send.at[t],
            recv_sem=rim_recv.at[t],
            device_id={"hist": lax.rem(me + last, count)},
            device_id_type=MESH,
        )

    def main_part(t):
        taps_copies[t].wait()
        for g in range(groups):
            span = BLOCK if g == groups - 1 else LENGTH
            taps_freq[g] = dot(ahead[:, :span], taps_buf[pl.ds(g * BLOCK, span), cols(t)])
        for b in range(seqs):
            hist_copies[t][b].wait()
            for g in range(groups):
                freq = dot(ahead[:, :BLOCK], hist_buf[b, pl.ds(g * BLOCK, BLOCK), cols(t)])
                if g == groups - 1:
                    last_freq[t, b] = freq
                else:
                    data_freq[g] = freq
            for r in range(0, HALF, STEP):
                real = imag = None
                upper, lower = pl.ds(r, STEP), pl.ds(HALF + r, STEP)
                for g in range(groups):
                    data = last_freq.at[t, b] if g == groups - 1 else data_freq.at[g]
                    tc, ts = taps_freq[g, upper, :], taps_freq[g, lower, :]
                    dc, ds = data[upper, :], data[lower, :]
                    re = tc * dc + ts * ds
                    im = tc * ds - ts * dc
                    real = re if real is None else real + re
                    imag = im if imag is None else imag + im
                mixed[upper, :] = real.astype(jnp.bfloat16)
                mixed[lower, :] = imag.astype(jnp.bfloat16)
            partial[t, b] = dot(back[...], mixed[...])

    def corner_part(t):
        taps_freq[0] = dot(ahead[:, BLOCK:], taps_buf[pl.ds(rows, NEW), cols(t)])
        for b in range(seqs):
            for r in range(0, HALF, STEP):
                upper, lower = pl.ds(r, STEP), pl.ds(HALF + r, STEP)
                tc, ts = taps_freq[0, upper, :], taps_freq[0, lower, :]
                dc, ds = last_freq[t, b, upper, :], last_freq[t, b, lower, :]
                mixed[upper, :] = (tc * dc + ts * ds).astype(jnp.bfloat16)
                mixed[lower, :] = (tc * ds - ts * dc).astype(jnp.bfloat16)
            partial[t, b] += dot(back[...], mixed[...])

    def skip_part(t):
        for b in range(seqs):
            newest = hist_buf[b, pl.ds(rows - NEW, NEW), cols(t)].astype(jnp.float32)
            partial[t, b] += skip_buf[:, cols(t)] * newest

    def pack(t):
        low = lax.rem(lax.broadcasted_iota(jnp.int32, (NEW, lanes), 0), 8) < 4
        evens, odds = [], []
        for b in range(0, seqs, 2):
            first, second = partial[t, b], partial[t, b + 1]
            evens.append(jnp.where(low, first, pltpu.roll(second, 4, 0)))
            odds.append(jnp.where(low, pltpu.roll(first, NEW - 4, 0), second))
        for d in range(count):
            source = odds if d % 2 else evens
            at = d // 2 * 8
            piece = jnp.concatenate([source[0][at : at + 8], source[1][at : at + 8]], axis=0)
            send_buf[d, :, cols(t)] = piece.astype(jnp.bfloat16)

    def send(d):
        return pltpu.make_async_remote_copy(
            src_ref=send_buf.at[d],
            dst_ref=recv_buf.at[me],
            send_sem=send_sem.at[d],
            recv_sem=recv_sem.at[me],
            device_id={"hist": d},
            device_id_type=MESH,
        )

    def arrival(d):
        return pltpu.make_async_remote_copy(
            src_ref=send_buf.at[d],
            dst_ref=recv_buf.at[d],
            send_sem=send_sem.at[d],
            recv_sem=recv_sem.at[d],
            device_id={"hist": d},
            device_id_type=MESH,
        )

    for copy in heads:
        copy.wait()

    def meet():
        @pl.when(place > 0)
        def _():
            pl.semaphore_wait(barrier, place)

        @pl.when(me > 1)
        def _():
            for t in range(tiles):
                rim(t).start()

        for spot, other in enumerate(order):

            @pl.when(spot < place)
            def _():
                pl.semaphore_signal(
                    ready_sem.at[me], inc=1, device_id={"hist": other}, device_id_type=MESH
                )

    @pl.when(me >= late)
    def _():
        meet()

    for copy in smalls:
        copy.wait()
    for t in range(tiles):
        main_part(t)

    @pl.when(me < late)
    def _():
        meet()

    @pl.when(me != last)
    def _():
        for t in range(tiles):
            rim(t).wait_recv()
            corner_part(t)

    @pl.when(me == last)
    def _():
        for t in range(tiles):
            skip_part(t)

    for t in range(tiles):
        pack(t)

    @pl.when(me >= late)
    def _():
        send(0).start()

    for spot, d in enumerate(order):

        @pl.when(place < spot)
        def _():
            pl.semaphore_wait(ready_sem.at[d], 1)

        if d == 0:

            @pl.when(me == 1)
            def _():
                for t in range(tiles):
                    rim(t).start()

            @pl.when(jnp.logical_and(me != 0, me < late))
            def _():
                send(0).start()

        else:

            @pl.when(me != d)
            def _():
                send(d).start()

    gate = jnp.concatenate([gate_buf[b].astype(jnp.float32) for b in range(seqs)], axis=0)
    recv_buf[me] = send_buf[me]
    total = None
    for d in range(count):

        @pl.when(me != d)
        def _():
            arrival(d).wait_recv()

        value = recv_buf[d].astype(jnp.float32)
        total = value if total is None else total + value
    result = (gate * total).astype(jnp.bfloat16)
    for b in range(seqs):
        output[b] = result[b * own : (b + 1) * own]

    @pl.when(me > 0)
    def _():
        for t in range(tiles):
            rim(t).wait_send()

    for d in range(count):

        @pl.when(me != d)
        def _():
            send(d).wait_send()


def body(history, filter_taps, skip_gain, gate_values):
    count = lax.axis_size("hist")
    seqs, rows, channels = history.shape
    own = gate_values.shape[1]
    lanes = min(256, channels)
    tiles = channels // lanes
    groups = rows // BLOCK
    ahead, back = tables()
    anywhere = pl.BlockSpec(memory_space=pl.ANY)
    f32, bf16 = jnp.float32, jnp.bfloat16
    return pl.pallas_call(
        functools.partial(kernel, lanes),
        out_shape=jax.ShapeDtypeStruct((seqs, own, channels), bf16),
        in_specs=[anywhere] * 6,
        out_specs=pl.BlockSpec(memory_space=pltpu.VMEM),
        scratch_shapes=[
            pltpu.VMEM((seqs, rows, channels), bf16),
            pltpu.VMEM((rows + NEW, channels), bf16),
            pltpu.VMEM((1, channels), f32),
            pltpu.VMEM((seqs, own, channels), bf16),
            pltpu.VMEM(ahead.shape, bf16),
            pltpu.VMEM(back.shape, bf16),
            pltpu.VMEM((groups, LENGTH, lanes), f32),
            pltpu.VMEM((groups - 1, LENGTH, lanes), f32),
            pltpu.VMEM((tiles, seqs, LENGTH, lanes), f32),
            pltpu.VMEM((LENGTH, lanes), bf16),
            pltpu.VMEM((tiles, seqs, NEW, lanes), f32),
            pltpu.VMEM((count, seqs * own, channels), bf16),
            pltpu.VMEM((count, seqs * own, channels), bf16),
            pltpu.SemaphoreType.DMA((tiles, seqs)),
            pltpu.SemaphoreType.DMA((tiles,)),
            pltpu.SemaphoreType.DMA((tiles,)),
            pltpu.SemaphoreType.DMA((4,)),
            pltpu.SemaphoreType.DMA((tiles,)),
            pltpu.SemaphoreType.DMA((tiles,)),
            pltpu.SemaphoreType.DMA((count,)),
            pltpu.SemaphoreType.DMA((count,)),
            pltpu.SemaphoreType.REGULAR((count,)),
        ],
        compiler_params=pltpu.CompilerParams(collective_id=0, has_side_effects=True),
        name="hyena_window",
    )(history, filter_taps, skip_gain.reshape(1, channels), gate_values, ahead, back)


def solution(mesh):
    placed = (
        P(("grp", "seq"), "hist", "chan"),
        P(("grp", "hist"), "chan"),
        P(("grp", "chan")),
        P(("grp", "seq"), "hist", "chan"),
    )
    return jax.shard_map(
        body,
        mesh=mesh,
        in_specs=placed,
        out_specs=P(("grp", "seq"), "hist", "chan"),
        check_vma=False,
    )
```

time: 68.6 us -> 62 us (0.904)
  Pallas kernels: 66.9 us -> 60.3 us
    pallas_call x1, Pallas kernels: 66.9 us -> 60.3 us  [body(): pl.pallas_call(functools.partial(kernel, lanes), out_shape=jax.ShapeDtype...]
    unnamed x2 -> x1, local copies, waits for them, and re-layouts: 0.01 us -> 1.33 us
    reshape x1 -> x0, local copies, waits for them, and re-layouts: 0.77 us -> none  [body(): summed.reshape(seqs, own, channels)]
where the time goes in v2:
time: 62 us; the launch traced here: 61.7 us
  Pallas kernels  60.3 us (97%)
  local copies, waits for them, and re-layouts  1.33 us (2%)
    pallas_call x1, Pallas kernels, body(): pl.pallas_call(functools.partial(kernel, lanes), out_shape=jax.ShapeDtype...  60.3 us
    unnamed x1, local copies, waits for them, and re-layouts  1.33 us

profile of v2, /device:TPU:80, one launch (start us, length us, event | category | flops | bytes accessed | tf_op | source)
XLA Modules:
  0.0 61.7 jit_solution(16755065486006874473)
XLA Ops:
  0.0 60.3 %hyena_window.1 = bf16[4,4,512]{2,1,0:T(4,128)(2,1)} custom-call(bf16[4,512,512]{2,1,0:T(8,128)(2,1)} %history.1, bf16[512,512]{1,0:T(8,128)(2,1)} %filter_taps.1, f32[1,512]{1,0:T(1,128)} %bitcast.1, bf16[4,4,512]{2,1,0:T(4,128)(2,1)} %gate_values.1, bf16[192,192]{1,0:T(8,128)(2,1)} %constant.4.clone.ahead_table, bf16[64,192]{1,0:T(8,128)(2,1)} %constant.5.clone.back_table), custom_call_target="tpu_custom_call" | custom-call | tf_op jit(solution)/shard_map/hyena_window/pallas_call | solution.py:332
  60.3 1.3 %copy.8 = bf16[4,4,512]{2,1,0:T(4,128)(2,1)} copy(bf16[4,4,512]{2,1,0:T(4,128)(2,1)} %hyena_window.1) | data formatting | bytes 32768

commit v3 on v2

v3 whole, which is shorter than its diff:
```python
import functools

import jax
import jax.numpy as jnp
import numpy as np
from jax import lax
from jax.experimental import pallas as pl
from jax.experimental.pallas import tpu as pltpu
from jax.sharding import PartitionSpec as P

NEW = 64
BLOCK = 128
LENGTH = BLOCK + NEW
HALF = LENGTH // 2
STEP = 16
LOWER = HALF + 8
PADDED = LOWER + HALF
MESH = pl.DeviceIdType.MESH


def tables():
    freqs = np.arange(HALF) + 0.5
    angle = 2.0 * np.pi / LENGTH * np.outer(freqs, np.arange(LENGTH))
    ahead = np.concatenate([np.cos(angle), np.sin(angle)], axis=0)
    lags = NEW - 1 - np.arange(NEW)
    angle = 2.0 * np.pi / LENGTH * np.outer(lags, freqs)
    back = np.concatenate([np.cos(angle), -np.sin(angle)], axis=1) * (2.0 / LENGTH)
    return jnp.asarray(ahead, jnp.bfloat16), jnp.asarray(back, jnp.bfloat16)


def dot(a, b):
    return jnp.dot(a, b, preferred_element_type=jnp.float32)


def kernel(
    lanes,
    history,
    filter_taps,
    skip_gain,
    gate_values,
    ahead_table,
    back_table,
    output,
    hist_buf,
    taps_buf,
    ahead,
    back,
    taps_freq,
    data_freq,
    last_freq,
    mixed,
    partial,
    send_buf,
    recv_buf,
    gate_buf,
    skip_buf,
    hist_sem,
    taps_sem,
    small_sem,
    rim_send,
    rim_recv,
    send_sem,
    recv_sem,
    ready_sem,
    zero_sem,
):
    count = lax.axis_size("hist")
    me = lax.axis_index("hist")
    seqs, rows, channels = hist_buf.shape
    own = NEW // count
    tiles = channels // lanes
    groups = rows // BLOCK
    last = count - 1

    beside = [i for i in range(1, count) if i <= 3 or i >= count - 3]
    relays = {i: 3 if i < 8 else 7 if i < 12 else 1 for i in range(1, count) if i not in beside}
    tail = range(count - 3, count)

    def is_in(group):
        found = me == group[0]
        for i in group[1:]:
            found = jnp.logical_or(found, me == i)
        return found

    is_beside = is_in(beside)

    def cols(t):
        if not isinstance(t, int):
            return pl.ds(pl.multiple_of(t * lanes, lanes), lanes)
        return pl.ds(t * lanes, lanes)

    def taps_copy(t):
        return pltpu.make_async_copy(
            filter_taps.at[:, cols(t)], taps_buf.at[pl.ds(0, rows), cols(t)], taps_sem.at[t]
        )

    def hist_copy(t, b):
        return pltpu.make_async_copy(
            history.at[b, :, cols(t)], hist_buf.at[b, :, cols(t)], hist_sem.at[t, b]
        )

    smalls = [
        pltpu.make_async_copy(source, target, small_sem.at[i])
        for i, (source, target) in enumerate(
            [
                (ahead_table, ahead),
                (back_table, back),
                (skip_gain, skip_buf),
                (gate_values, gate_buf),
            ]
        )
    ]
    barrier = pltpu.get_barrier_semaphore()

    def rim(t):
        return pltpu.make_async_remote_copy(
            src_ref=filter_taps.at[pl.ds(0, NEW), cols(t)],
            dst_ref=taps_buf.at[pl.ds(rows, NEW), cols(t)],
            send_sem=rim_send.at[t],
            recv_sem=rim_recv.at[t],
            device_id={"hist": lax.rem(me + last, count)},
            device_id_type=MESH,
        )

    def keep(ref, freq):
        ref[:HALF, :] = freq[:HALF]
        ref[LOWER:, :] = freq[HALF:]

    def main_part(t):
        taps_copy(t).wait()
        for g in range(groups):
            span = BLOCK if g == groups - 1 else LENGTH
            keep(taps_freq.at[g], dot(ahead[:, :span], taps_buf[pl.ds(g * BLOCK, span), cols(t)]))
        for b in range(seqs):
            hist_copy(t, b).wait()
            for g in range(groups):
                freq = dot(ahead[:, :BLOCK], hist_buf[b, pl.ds(g * BLOCK, BLOCK), cols(t)])
                if g == groups - 1:
                    keep(last_freq.at[t, b], freq)
                else:
                    keep(data_freq.at[b % 2, g], freq)
            for r in range(0, HALF, STEP):
                real = imag = None
                upper, lower, under = pl.ds(r, STEP), pl.ds(LOWER + r, STEP), pl.ds(HALF + r, STEP)
                for g in range(groups):
                    data = last_freq.at[t, b] if g == groups - 1 else data_freq.at[b % 2, g]
                    tc, ts = taps_freq[g, upper, :], taps_freq[g, lower, :]
                    dc, ds = data[upper, :], data[lower, :]
                    re = tc * dc + ts * ds
                    im = tc * ds - ts * dc
                    real = re if real is None else real + re
                    imag = im if imag is None else imag + im
                mixed[b % 2, upper, :] = real.astype(jnp.bfloat16)
                mixed[b % 2, under, :] = imag.astype(jnp.bfloat16)
            partial[t, b] = dot(back[...], mixed[b % 2])

    def corner_part(t):
        keep(taps_freq.at[0], dot(ahead[:, BLOCK:], taps_buf[pl.ds(rows, NEW), cols(t)]))
        for b in range(seqs):
            for r in range(0, HALF, STEP):
                upper, lower, under = pl.ds(r, STEP), pl.ds(LOWER + r, STEP), pl.ds(HALF + r, STEP)
                tc, ts = taps_freq[0, upper, :], taps_freq[0, lower, :]
                dc, ds = last_freq[t, b, upper, :], last_freq[t, b, lower, :]
                mixed[b % 2, upper, :] = (tc * dc + ts * ds).astype(jnp.bfloat16)
                mixed[b % 2, under, :] = (tc * ds - ts * dc).astype(jnp.bfloat16)
            partial[t, b] += dot(back[...], mixed[b % 2])

    def skip_part(t):
        for b in range(seqs):
            newest = hist_buf[b, pl.ds(rows - NEW, NEW), cols(t)].astype(jnp.float32)
            partial[t, b] += skip_buf[:, cols(t)] * newest

    def pack(t):
        low = lax.rem(lax.broadcasted_iota(jnp.int32, (NEW, lanes), 0), 8) < 4
        evens, odds = [], []
        for b in range(0, seqs, 2):
            first, second = partial[t, b], partial[t, b + 1]
            evens.append(jnp.where(low, first, pltpu.roll(second, 4, 0)))
            odds.append(jnp.where(low, pltpu.roll(first, NEW - 4, 0), second))
        for d in range(count):
            source = odds if d % 2 else evens
            at = d // 2 * 8
            piece = jnp.concatenate([source[0][at : at + 8], source[1][at : at + 8]], axis=0)
            send_buf[d, :, cols(t)] = piece.astype(jnp.bfloat16)

    def send(d):
        return pltpu.make_async_remote_copy(
            src_ref=send_buf.at[d],
            dst_ref=recv_buf.at[me],
            send_sem=send_sem.at[d],
            recv_sem=recv_sem.at[me],
            device_id={"hist": d},
            device_id_type=MESH,
        )

    def arrival(d):
        return pltpu.make_async_remote_copy(
            src_ref=send_buf.at[d],
            dst_ref=recv_buf.at[d],
            send_sem=send_sem.at[d],
            recv_sem=recv_sem.at[d],
            device_id={"hist": d},
            device_id_type=MESH,
        )

    def greet():
        for other in range(1, count):
            told = jnp.logical_and(me > 0, me < other)
            if other in beside:
                told = me < other

            @pl.when(told)
            def _():
                pl.semaphore_signal(barrier, inc=1, device_id={"hist": other}, device_id_type=MESH)

    def tell_ready(other):
        pl.semaphore_signal(
            ready_sem.at[me], inc=1, device_id={"hist": other}, device_id_type=MESH
        )

    def meet():
        pl.semaphore_wait(barrier, me - jnp.where(is_beside, 0, 1))
        for t in range(tiles):
            rim(t).start()

        @pl.when(is_beside)
        def _():
            tell_ready(0)

        for other in range(1, count - 1):

            @pl.when(other < me)
            def _():
                tell_ready(other)

    smalls[0].start()
    smalls[1].start()
    taps_copy(0).start()
    for b in range(seqs // 2):
        hist_copy(0, b).start()

    with jax.named_scope("greet"):
        greet()

    with jax.named_scope("meet"):

        @pl.when(me != 0)
        def _():
            meet()

    with jax.named_scope("loads"):
        for b in range(seqs // 2, seqs):
            hist_copy(0, b).start()
        for t in range(1, tiles):
            taps_copy(t).start()
            for b in range(seqs):
                hist_copy(t, b).start()
        for copy in smalls[2:]:
            copy.start()

    with jax.named_scope("ahead"):
        smalls[0].wait()
        smalls[1].wait()
    @pl.loop(0, tiles)
    def _(t):
        with jax.named_scope("main"):
            main_part(t)

    @pl.when(me != last)
    def _():
        @pl.loop(0, tiles)
        def _(t):
            with jax.named_scope("rim_wait"):
                rim(t).wait_recv()
            with jax.named_scope("corner"):
                corner_part(t)

    with jax.named_scope("skip"):
        smalls[2].wait()
        smalls[3].wait()

        @pl.when(me == last)
        def _():
            for t in range(tiles):
                skip_part(t)

    with jax.named_scope("pack"):
        for t in range(tiles):
            pack(t)

    def ready(d):
        with jax.named_scope("ready"):

            @pl.when(me < d)
            def _():
                pl.semaphore_wait(ready_sem.at[d], 1)

    def relay(d):
        if d in relays:

            @pl.when(me == relays[d])
            def _():
                pl.semaphore_signal(zero_sem, inc=1, device_id={"hist": d}, device_id_type=MESH)

    is_late = me >= count - 2
    singly = 2

    @pl.when(is_beside)
    def _():
        send(0).start()

    @pl.when(is_late)
    def _():
        send(0).wait_send()

    is_between = jnp.logical_not(jnp.logical_or(is_beside, me == 0))

    @pl.when(is_between)
    def _():
        for d in range(1, 4):
            send(d).start()

    with jax.named_scope("zero"):

        @pl.when(is_between)
        def _():
            pl.semaphore_wait(zero_sem, 1)
            tell_ready(0)
            send(0).start()

    for d in range(1, count):
        if d in tail:
            now = jnp.logical_or(me == 0, me > d)

            @pl.when(now)
            def _():
                ready(d)

        else:
            now = me != d
            if d < 4:
                now = jnp.logical_and(now, jnp.logical_not(is_between))
            ready(d)
            relay(d)

        @pl.when(now)
        def _():
            send(d).start()

        if d < singly:

            @pl.when(is_late)
            def _():
                send(d).wait_send()

    def arrive(d):
        with jax.named_scope("arrive"):

            @pl.when(me != d)
            def _():
                arrival(d).wait_recv()

    arrive(last - 2)
    for d in tail:

        @pl.when(jnp.logical_and(me > 0, me < d))
        def _():
            ready(d)
            send(d).start()

    gate = jnp.concatenate([gate_buf[b].astype(jnp.float32) for b in range(seqs)], axis=0)
    recv_buf[me] = send_buf[me]
    total = None
    for d in range(count):
        if d != last - 2:
            arrive(d)
        value = recv_buf[d].astype(jnp.float32)
        total = value if total is None else total + value
    result = (gate * total).astype(jnp.bfloat16)
    for b in range(seqs):
        output[b] = result[b * own : (b + 1) * own]

    with jax.named_scope("drain"):

        @pl.when(me > 0)
        def _():
            for t in range(tiles):
                rim(t).wait_send()

        for d in range(count):
            left = me != d
            if d < singly:
                left = jnp.logical_and(left, jnp.logical_not(is_late))

            @pl.when(left)
            def _():
                send(d).wait_send()


def body(history, filter_taps, skip_gain, gate_values):
    count = lax.axis_size("hist")
    seqs, rows, channels = history.shape
    own = gate_values.shape[1]
    lanes = min(256, channels)
    tiles = channels // lanes
    groups = rows // BLOCK
    ahead, back = tables()
    anywhere = pl.BlockSpec(memory_space=pl.ANY)
    f32, bf16 = jnp.float32, jnp.bfloat16
    return pl.pallas_call(
        functools.partial(kernel, lanes),
        out_shape=pltpu.VMEM((seqs, own, channels), bf16),
        in_specs=[anywhere] * 6,
        out_specs=pl.BlockSpec(memory_space=pltpu.VMEM),
        scratch_shapes=[
            pltpu.VMEM((seqs, rows, channels), bf16),
            pltpu.VMEM((rows + NEW, channels), bf16),
            pltpu.VMEM(ahead.shape, bf16),
            pltpu.VMEM(back.shape, bf16),
            pltpu.VMEM((groups, PADDED, lanes), f32),
            pltpu.VMEM((2, groups - 1, PADDED, lanes), f32),
            pltpu.VMEM((tiles, seqs, PADDED, lanes), f32),
            pltpu.VMEM((2, LENGTH, lanes), bf16),
            pltpu.VMEM((tiles, seqs, NEW, lanes), f32),
            pltpu.VMEM((count, seqs * own, channels), bf16),
            pltpu.VMEM((count, seqs * own, channels), bf16),
            pltpu.VMEM((seqs, own, channels), bf16),
            pltpu.VMEM((1, channels), f32),
            pltpu.SemaphoreType.DMA((tiles, seqs)),
            pltpu.SemaphoreType.DMA((tiles,)),
            pltpu.SemaphoreType.DMA((4,)),
            pltpu.SemaphoreType.DMA((tiles,)),
            pltpu.SemaphoreType.DMA((tiles,)),
            pltpu.SemaphoreType.DMA((count,)),
            pltpu.SemaphoreType.DMA((count,)),
            pltpu.SemaphoreType.REGULAR((count,)),
            pltpu.SemaphoreType.REGULAR,
        ],
        compiler_params=pltpu.CompilerParams(collective_id=0, has_side_effects=True),
        name="hyena_window",
    )(history, filter_taps, skip_gain.reshape(1, channels), gate_values, ahead, back)


def solution(mesh):
    placed = (
        P(("grp", "seq"), "hist", "chan"),
        P(("grp", "hist"), "chan"),
        P(("grp", "chan")),
        P(("grp", "seq"), "hist", "chan"),
    )
    return jax.shard_map(
        body,
        mesh=mesh,
        in_specs=placed,
        out_specs=P(("grp", "seq"), "hist", "chan"),
        check_vma=False,
    )
```

time: 62 us -> 54.1 us (0.87)
  the two profiles are of different devices: /device:TPU:80 before, /device:TPU:192 now
where the time goes in v3:
time: 54.1 us; the launch traced here: 54 us
  Pallas kernels  53.3 us (99%)
  local copies, waits for them, and re-layouts  0.61 us (1%)
    pallas_call x1, Pallas kernels, body(): pl.pallas_call(functools.partial(kernel, lanes), out_shape=pltpu.VMEM((se...  53.3 us

profile of v3, /device:TPU:192, one launch (start us, length us, event | category | flops | bytes accessed | tf_op | source)
XLA Modules:
  0.0 54.0 jit_solution(2082637963194290117)
XLA Ops:
  0.0 53.3 %hyena_window.1 = bf16[4,4,512]{2,1,0:T(4,128)(2,1)S(1)} custom-call(bf16[4,512,512]{2,1,0:T(8,128)(2,1)} %history.1, bf16[512,512]{1,0:T(8,128)(2,1)} %filter_taps.1, f32[1,512]{1,0:T(1,128)} %bitcast.1, bf16[4,4,512]{2,1,0:T(4,128)(2,1)} %gate_values.1, bf16[192,192]{1,0:T(8,128)(2,1)} %constant.4.clone.ahead_table, bf16[64,192]{1,0:T(8,128)(2,1)} %constant.5.clone.back_table), custom_call_target="tpu_custom_call" | custom-call | tf_op jit(solution)/shard_map/hyena_window/pallas_call | solution.py:410
  53.4 0.6 %copy.8 = bf16[4,4,512]{2,1,0:T(4,128)(2,1)} copy(bf16[4,4,512]{2,1,0:T(4,128)(2,1)S(1)} %hyena_window.1) | data formatting | bytes 32768

commit v4 on v3

--- a/solution.py
+++ b/solution.py
@@ -13,8 +13,6 @@
 LENGTH = BLOCK + NEW
 HALF = LENGTH // 2
 STEP = 16
-LOWER = HALF + 8
-PADDED = LOWER + HALF
 MESH = pl.DeviceIdType.MESH
 
 
@@ -34,6 +32,7 @@
 
 def kernel(
     lanes,
+    parts,
     history,
     filter_taps,
     skip_gain,
@@ -112,58 +111,66 @@
     ]
     barrier = pltpu.get_barrier_semaphore()
 
-    def rim(t):
+    cores = lax.axis_size("seq")
+    core = lax.axis_index("seq")
+    sender = cores - 1
+    width = channels // parts
+
+    def rim(p, target):
+        lane = pl.ds(p * width, width)
         return pltpu.make_async_remote_copy(
-            src_ref=filter_taps.at[pl.ds(0, NEW), cols(t)],
-            dst_ref=taps_buf.at[pl.ds(rows, NEW), cols(t)],
-            send_sem=rim_send.at[t],
-            recv_sem=rim_recv.at[t],
-            device_id={"hist": lax.rem(me + last, count)},
+            src_ref=filter_taps.at[pl.ds(0, NEW), lane],
+            dst_ref=taps_buf.at[pl.ds(rows, NEW), lane],
+            send_sem=rim_send.at[p, target],
+            recv_sem=rim_recv.at[p],
+            device_id={"hist": lax.rem(me + last, count), "seq": target},
             device_id_type=MESH,
         )
 
-    def keep(ref, freq):
-        ref[:HALF, :] = freq[:HALF]
-        ref[LOWER:, :] = freq[HALF:]
+    def sends_rim(target):
+        return jnp.where(me > 1, core == sender, jnp.logical_and(me == 1, core == target))
 
     def main_part(t):
         taps_copy(t).wait()
         for g in range(groups):
             span = BLOCK if g == groups - 1 else LENGTH
-            keep(taps_freq.at[g], dot(ahead[:, :span], taps_buf[pl.ds(g * BLOCK, span), cols(t)]))
+            taps_freq[g] = dot(ahead[:, :span], taps_buf[pl.ds(g * BLOCK, span), cols(t)])
         for b in range(seqs):
             hist_copy(t, b).wait()
             for g in range(groups):
                 freq = dot(ahead[:, :BLOCK], hist_buf[b, pl.ds(g * BLOCK, BLOCK), cols(t)])
                 if g == groups - 1:
-                    keep(last_freq.at[t, b], freq)
+                    last_freq[t, b] = freq
                 else:
-                    keep(data_freq.at[b % 2, g], freq)
+                    data_freq[b, g] = freq
             for r in range(0, HALF, STEP):
                 real = imag = None
-                upper, lower, under = pl.ds(r, STEP), pl.ds(LOWER + r, STEP), pl.ds(HALF + r, STEP)
+                upper, lower = pl.ds(r, STEP), pl.ds(HALF + r, STEP)
                 for g in range(groups):
-                    data = last_freq.at[t, b] if g == groups - 1 else data_freq.at[b % 2, g]
+                    data = last_freq.at[t, b] if g == groups - 1 else data_freq.at[b, g]
                     tc, ts = taps_freq[g, upper, :], taps_freq[g, lower, :]
                     dc, ds = data[upper, :], data[lower, :]
                     re = tc * dc + ts * ds
                     im = tc * ds - ts * dc
                     real = re if real is None else real + re
                     imag = im if imag is None else imag + im
-                mixed[b % 2, upper, :] = real.astype(jnp.bfloat16)
-                mixed[b % 2, under, :] = imag.astype(jnp.bfloat16)
-            partial[t, b] = dot(back[...], mixed[b % 2])
-
-    def corner_part(t):
-        keep(taps_freq.at[0], dot(ahead[:, BLOCK:], taps_buf[pl.ds(rows, NEW), cols(t)]))
+                mixed[b, upper, :] = real.astype(jnp.bfloat16)
+                mixed[b, lower, :] = imag.astype(jnp.bfloat16)
+        for b in range(seqs):
+            partial[t, b] = dot(back[...], mixed[b])
+
+    def corner_part(p):
+        lane = pl.ds(p * width, width)
+        taps_freq[0, :, lane] = dot(ahead[:, BLOCK:], taps_buf[pl.ds(rows, NEW), lane])
         for b in range(seqs):
             for r in range(0, HALF, STEP):
-                upper, lower, under = pl.ds(r, STEP), pl.ds(LOWER + r, STEP), pl.ds(HALF + r, STEP)
-                tc, ts = taps_freq[0, upper, :], taps_freq[0, lower, :]
-                dc, ds = last_freq[t, b, upper, :], last_freq[t, b, lower, :]
-                mixed[b % 2, upper, :] = (tc * dc + ts * ds).astype(jnp.bfloat16)
-                mixed[b % 2, under, :] = (tc * ds - ts * dc).astype(jnp.bfloat16)
-            partial[t, b] += dot(back[...], mixed[b % 2])
+                upper, lower = pl.ds(r, STEP), pl.ds(HALF + r, STEP)
+                tc, ts = taps_freq[0, upper, lane], taps_freq[0, lower, lane]
+                dc, ds = last_freq[0, b, upper, lane], last_freq[0, b, lower, lane]
+                mixed[b, upper, lane] = (tc * dc + ts * ds).astype(jnp.bfloat16)
+                mixed[b, lower, lane] = (tc * ds - ts * dc).astype(jnp.bfloat16)
+        for b in range(seqs):
+            partial[0, b, :, lane] += dot(back[...], mixed[b, :, lane])
 
     def skip_part(t):
         for b in range(seqs):
@@ -213,15 +220,32 @@
             def _():
                 pl.semaphore_signal(barrier, inc=1, device_id={"hist": other}, device_id_type=MESH)
 
+        for other in range(cores - 1):
+
+            @pl.when(jnp.logical_and(core == other, jnp.logical_and(me > 0, me < last)))
+            def _():
+                pl.semaphore_signal(
+                    barrier,
+                    inc=1,
+                    device_id={"hist": lax.rem(me + 1, count), "seq": sender},
+                    device_id_type=MESH,
+                )
+
     def tell_ready(other):
         pl.semaphore_signal(
             ready_sem.at[me], inc=1, device_id={"hist": other}, device_id_type=MESH
         )
 
     def meet():
-        pl.semaphore_wait(barrier, me - jnp.where(is_beside, 0, 1))
-        for t in range(tiles):
-            rim(t).start()
+        others = jnp.where(jnp.logical_and(core == sender, me > 1), cores - 1, 0)
+        pl.semaphore_wait(barrier, me - jnp.where(is_beside, 0, 1) + others)
+
+        for target in range(cores):
+
+            @pl.when(sends_rim(target))
+            def _():
+                for p in range(parts):
+                    rim(p, target).start()
 
         @pl.when(is_beside)
         def _():
@@ -268,12 +292,11 @@
 
     @pl.when(me != last)
     def _():
-        @pl.loop(0, tiles)
-        def _(t):
+        for p in range(parts):
             with jax.named_scope("rim_wait"):
-                rim(t).wait_recv()
+                rim(p, 0).wait_recv()
             with jax.named_scope("corner"):
-                corner_part(t)
+                corner_part(p)
 
     with jax.named_scope("skip"):
         smalls[2].wait()
@@ -315,9 +338,17 @@
 
     is_between = jnp.logical_not(jnp.logical_or(is_beside, me == 0))
 
-    @pl.when(is_between)
-    def _():
-        for d in range(1, 4):
+    first = range(1, 5)
+    held_from = count - 4
+    is_held = me >= held_from
+
+    for d in range(1, held_from):
+        early = jnp.logical_and(is_between, d < me)
+        if d not in first:
+            early = jnp.logical_and(early, jnp.logical_not(is_held))
+
+        @pl.when(early)
+        def _():
             send(d).start()
 
     with jax.named_scope("zero"):
@@ -328,39 +359,58 @@
             tell_ready(0)
             send(0).start()
 
-    for d in range(1, count):
+    def arrive(d):
+        with jax.named_scope("arrive"):
+            arrival(d).wait_recv()
+
+    for d in first:
+        ready(d)
+        relay(d)
+
+        @pl.when(jnp.logical_and(me != d, jnp.logical_not(is_between)))
+        def _():
+            send(d).start()
+
+        if d < singly:
+
+            @pl.when(is_late)
+            def _():
+                send(d).wait_send()
+
+    @pl.when(me == last)
+    def _():
+        for d in range(held_from, last):
+            send(d).start()
+        arrive(last - 1)
+
+    @pl.when(jnp.logical_and(is_held, me != last))
+    def _():
+        arrive(last)
+
+    for d in range(first[-1] + 1, count):
+        now = me != d
         if d in tail:
             now = jnp.logical_or(me == 0, me > d)
-
-            @pl.when(now)
-            def _():
-                ready(d)
-
+        if d >= held_from:
+            now = jnp.logical_and(now, me != last)
         else:
-            now = me != d
-            if d < 4:
-                now = jnp.logical_and(now, jnp.logical_not(is_between))
+            sent = jnp.logical_and(jnp.logical_and(is_between, jnp.logical_not(is_held)), d < me)
+            now = jnp.logical_and(now, jnp.logical_not(sent))
+
+        @pl.when(jnp.logical_and(now, me < d))
+        def _():
             ready(d)
-            relay(d)
+
+        relay(d)
 
         @pl.when(now)
         def _():
             send(d).start()
 
-        if d < singly:
-
-            @pl.when(is_late)
-            def _():
-                send(d).wait_send()
-
-    def arrive(d):
-        with jax.named_scope("arrive"):
-
-            @pl.when(me != d)
-            def _():
-                arrival(d).wait_recv()
-
-    arrive(last - 2)
+    @pl.when(me != last - 2)
+    def _():
+        arrive(last - 2)
+
     for d in tail:
 
         @pl.when(jnp.logical_and(me > 0, me < d))
@@ -372,8 +422,17 @@
     recv_buf[me] = send_buf[me]
     total = None
     for d in range(count):
+        due = me != d
+        if d == last - 1:
+            due = jnp.logical_and(due, me != last)
+        if d == last:
+            due = me < held_from
         if d != last - 2:
-            arrive(d)
+
+            @pl.when(due)
+            def _():
+                arrive(d)
+
         value = recv_buf[d].astype(jnp.float32)
         total = value if total is None else total + value
     result = (gate * total).astype(jnp.bfloat16)
@@ -382,10 +441,12 @@
 
     with jax.named_scope("drain"):
 
-        @pl.when(me > 0)
-        def _():
-            for t in range(tiles):
-                rim(t).wait_send()
+        for target in range(cores):
+
+            @pl.when(sends_rim(target))
+            def _():
+                for p in range(parts):
+                    rim(p, target).wait_send()
 
         for d in range(count):
             left = me != d
@@ -401,14 +462,16 @@
     count = lax.axis_size("hist")
     seqs, rows, channels = history.shape
     own = gate_values.shape[1]
-    lanes = min(256, channels)
+    lanes = min(512, channels)
     tiles = channels // lanes
+    parts = max(channels // 256, 1)
     groups = rows // BLOCK
+    cores = lax.axis_size("seq")
     ahead, back = tables()
     anywhere = pl.BlockSpec(memory_space=pl.ANY)
     f32, bf16 = jnp.float32, jnp.bfloat16
     return pl.pallas_call(
-        functools.partial(kernel, lanes),
+        functools.partial(kernel, lanes, parts),
         out_shape=pltpu.VMEM((seqs, own, channels), bf16),
         in_specs=[anywhere] * 6,
         out_specs=pl.BlockSpec(memory_space=pltpu.VMEM),
@@ -417,10 +480,10 @@
             pltpu.VMEM((rows + NEW, channels), bf16),
             pltpu.VMEM(ahead.shape, bf16),
             pltpu.VMEM(back.shape, bf16),
-            pltpu.VMEM((groups, PADDED, lanes), f32),
-            pltpu.VMEM((2, groups - 1, PADDED, lanes), f32),
-            pltpu.VMEM((tiles, seqs, PADDED, lanes), f32),
-            pltpu.VMEM((2, LENGTH, lanes), bf16),
+            pltpu.VMEM((groups, LENGTH, lanes), f32),
+            pltpu.VMEM((seqs, groups - 1, LENGTH, lanes), f32),
+            pltpu.VMEM((tiles, seqs, LENGTH, lanes), f32),
+            pltpu.VMEM((seqs, LENGTH, lanes), bf16),
             pltpu.VMEM((tiles, seqs, NEW, lanes), f32),
             pltpu.VMEM((count, seqs * own, channels), bf16),
             pltpu.VMEM((count, seqs * own, channels), bf16),
@@ -429,8 +492,8 @@
             pltpu.SemaphoreType.DMA((tiles, seqs)),
             pltpu.SemaphoreType.DMA((tiles,)),
             pltpu.SemaphoreType.DMA((4,)),
-            pltpu.SemaphoreType.DMA((tiles,)),
-            pltpu.SemaphoreType.DMA((tiles,)),
+            pltpu.SemaphoreType.DMA((parts, cores)),
+            pltpu.SemaphoreType.DMA((parts,)),
             pltpu.SemaphoreType.DMA((count,)),
             pltpu.SemaphoreType.DMA((count,)),
             pltpu.SemaphoreType.REGULAR((count,)),

time: 54.1 us -> 52.2 us (0.965)
  Pallas kernels: 53.3 us -> 51.5 us
    pallas_call x1, Pallas kernels: 53.3 us -> 51.5 us  [body(): pl.pallas_call(functools.partial(kernel, lanes, parts), out_shape=pltpu.V...]
where the time goes in v4:
time: 52.2 us; the launch traced here: 52.1 us
  Pallas kernels  51.5 us (99%)
  local copies, waits for them, and re-layouts  0.61 us (1%)
    pallas_call x1, Pallas kernels, body(): pl.pallas_call(functools.partial(kernel, lanes, parts), out_shape=pltpu.V...  51.5 us

profile of v4, /device:TPU:192, one launch (start us, length us, event | category | flops | bytes accessed | tf_op | source)
XLA Modules:
  0.0 52.1 jit_solution(11419070096071553477)
XLA Ops:
  0.0 51.5 %hyena_window.1 = bf16[4,4,512]{2,1,0:T(4,128)(2,1)S(1)} custom-call(bf16[4,512,512]{2,1,0:T(8,128)(2,1)} %history.1, bf16[512,512]{1,0:T(8,128)(2,1)} %filter_taps.1, f32[1,512]{1,0:T(1,128)} %bitcast.1, bf16[4,4,512]{2,1,0:T(4,128)(2,1)} %gate_values.1, bf16[192,192]{1,0:T(8,128)(2,1)} %constant.4.clone.ahead_table, bf16[64,192]{1,0:T(8,128)(2,1)} %constant.5.clone.back_table), custom_call_target="tpu_custom_call" | custom-call | tf_op jit(solution)/shard_map/hyena_window/pallas_call | solution.py:473
  51.5 0.6 %copy.8 = bf16[4,4,512]{2,1,0:T(4,128)(2,1)} copy(bf16[4,4,512]{2,1,0:T(4,128)(2,1)S(1)} %hyena_window.1) | data formatting | bytes 32768

commit v5 on v4

--- a/solution.py
+++ b/solution.py
@@ -190,22 +190,25 @@
             piece = jnp.concatenate([source[0][at : at + 8], source[1][at : at + 8]], axis=0)
             send_buf[d, :, cols(t)] = piece.astype(jnp.bfloat16)
 
+    last_early = count - 5
+    singles = 2
+
     def send(d):
         return pltpu.make_async_remote_copy(
             src_ref=send_buf.at[d],
             dst_ref=recv_buf.at[me],
-            send_sem=send_sem.at[d],
-            recv_sem=recv_sem.at[me],
+            send_sem=send_sem.at[min(d, singles)],
+            recv_sem=recv_sem.at[jnp.maximum(me - last_early, 0)],
             device_id={"hist": d},
             device_id_type=MESH,
         )
 
-    def arrival(d):
+    def arrival(d, n=1):
         return pltpu.make_async_remote_copy(
-            src_ref=send_buf.at[d],
-            dst_ref=recv_buf.at[d],
-            send_sem=send_sem.at[d],
-            recv_sem=recv_sem.at[d],
+            src_ref=send_buf.at[pl.ds(d, n)],
+            dst_ref=recv_buf.at[pl.ds(d, n)],
+            send_sem=send_sem.at[min(d, singles)],
+            recv_sem=recv_sem.at[max(d - last_early, 0)],
             device_id={"hist": d},
             device_id_type=MESH,
         )
@@ -247,6 +250,10 @@
                 for p in range(parts):
                     rim(p, target).start()
 
+        @pl.when(core == sender)
+        def _():
+            load()
+
         @pl.when(is_beside)
         def _():
             tell_ready(0)
@@ -257,30 +264,27 @@
             def _():
                 tell_ready(other)
 
-    smalls[0].start()
-    smalls[1].start()
-    taps_copy(0).start()
-    for b in range(seqs // 2):
-        hist_copy(0, b).start()
-
-    with jax.named_scope("greet"):
-        greet()
-
-    with jax.named_scope("meet"):
-
-        @pl.when(me != 0)
-        def _():
-            meet()
-
-    with jax.named_scope("loads"):
-        for b in range(seqs // 2, seqs):
-            hist_copy(0, b).start()
-        for t in range(1, tiles):
+    def load():
+        smalls[0].start()
+        for t in range(tiles):
             taps_copy(t).start()
             for b in range(seqs):
                 hist_copy(t, b).start()
-        for copy in smalls[2:]:
+        for copy in smalls[1:]:
             copy.start()
+
+    @pl.when(jnp.logical_or(core != sender, me == 0))
+    def _():
+        load()
+
+    with jax.named_scope("greet"):
+        greet()
+
+    with jax.named_scope("meet"):
+
+        @pl.when(me != 0)
+        def _():
+            meet()
 
     with jax.named_scope("ahead"):
         smalls[0].wait()
@@ -367,7 +371,11 @@
         ready(d)
         relay(d)
 
-        @pl.when(jnp.logical_and(me != d, jnp.logical_not(is_between)))
+        now = jnp.logical_and(me != d, jnp.logical_not(is_between))
+        if d == first[-1]:
+            now = jnp.logical_and(now, me != held_from + 1)
+
+        @pl.when(now)
         def _():
             send(d).start()
 
@@ -386,6 +394,10 @@
     @pl.when(jnp.logical_and(is_held, me != last))
     def _():
         arrive(last)
+
+    @pl.when(me == held_from + 1)
+    def _():
+        send(first[-1]).start()
 
     for d in range(first[-1] + 1, count):
         now = me != d
@@ -407,7 +419,11 @@
         def _():
             send(d).start()
 
-    @pl.when(me != last - 2)
+    @pl.when(me == 1)
+    def _():
+        arrive(held_from)
+
+    @pl.when(jnp.logical_and(me != 1, me != last - 2))
     def _():
         arrive(last - 2)
 
@@ -421,13 +437,24 @@
     gate = jnp.concatenate([gate_buf[b].astype(jnp.float32) for b in range(seqs)], axis=0)
     recv_buf[me] = send_buf[me]
     total = None
+    with jax.named_scope("early"):
+        for missing in range(2):
+
+            @pl.when((me <= last_early) == bool(missing))
+            def _():
+                arrival(0, last_early + 1 - missing).wait_recv()
+
     for d in range(count):
         due = me != d
+        if d == held_from:
+            due = jnp.logical_and(due, me != 1)
+        if d == last - 2:
+            due = me == 1
         if d == last - 1:
             due = jnp.logical_and(due, me != last)
         if d == last:
             due = me < held_from
-        if d != last - 2:
+        if d > last_early:
 
             @pl.when(due)
             def _():
@@ -448,7 +475,7 @@
                 for p in range(parts):
                     rim(p, target).wait_send()
 
-        for d in range(count):
+        for d in range(singles):
             left = me != d
             if d < singly:
                 left = jnp.logical_and(left, jnp.logical_not(is_late))
@@ -456,6 +483,12 @@
             @pl.when(left)
             def _():
                 send(d).wait_send()
+
+        for missing in range(2):
+
+            @pl.when((me >= singles) == bool(missing))
+            def _():
+                arrival(singles, count - singles - missing).wait_send()
 
 
 def body(history, filter_taps, skip_gain, gate_values):
@@ -494,8 +527,8 @@
             pltpu.SemaphoreType.DMA((4,)),
             pltpu.SemaphoreType.DMA((parts, cores)),
             pltpu.SemaphoreType.DMA((parts,)),
-            pltpu.SemaphoreType.DMA((count,)),
-            pltpu.SemaphoreType.DMA((count,)),
+            pltpu.SemaphoreType.DMA((3,)),
+            pltpu.SemaphoreType.DMA((5,)),
             pltpu.SemaphoreType.REGULAR((count,)),
             pltpu.SemaphoreType.REGULAR,
         ],

time: 52.2 us -> 51.3 us (0.983)
  the two profiles are of different devices: /device:TPU:192 before, /device:TPU:80 now
where the time goes in v5:
time: 51.3 us; the launch traced here: 50.7 us
  Pallas kernels  50.1 us (98%)
  local copies, waits for them, and re-layouts  0.61 us (1%)
    pallas_call x1, Pallas kernels, body(): pl.pallas_call(functools.partial(kernel, lanes, parts), out_shape=pltpu.V...  50.1 us

profile of v5, /device:TPU:80, one launch (start us, length us, event | category | flops | bytes accessed | tf_op | source)
XLA Modules:
  0.0 50.7 jit_solution(6722799755463558620)
XLA Ops:
  0.0 50.1 %hyena_window.1 = bf16[4,4,512]{2,1,0:T(4,128)(2,1)S(1)} custom-call(bf16[4,512,512]{2,1,0:T(8,128)(2,1)} %history.1, bf16[512,512]{1,0:T(8,128)(2,1)} %filter_taps.1, f32[1,512]{1,0:T(1,128)} %bitcast.1, bf16[4,4,512]{2,1,0:T(4,128)(2,1)} %gate_values.1, bf16[192,192]{1,0:T(8,128)(2,1)} %constant.4.clone.ahead_table, bf16[64,192]{1,0:T(8,128)(2,1)} %constant.5.clone.back_table), custom_call_target="tpu_custom_call" | custom-call | tf_op jit(solution)/shard_map/hyena_window/pallas_call | solution.py:506
  50.1 0.6 %copy.8 = bf16[4,4,512]{2,1,0:T(4,128)(2,1)} copy(bf16[4,4,512]{2,1,0:T(4,128)(2,1)S(1)} %hyena_window.1) | data formatting | bytes 32768

commit v6 on v5

--- a/solution.py
+++ b/solution.py
@@ -497,7 +497,7 @@
     own = gate_values.shape[1]
     lanes = min(512, channels)
     tiles = channels // lanes
-    parts = max(channels // 256, 1)
+    parts = 1
     groups = rows // BLOCK
     cores = lax.axis_size("seq")
     ahead, back = tables()

time: 51.3 us -> 51.3 us (level)
  no operation moved by 1% of the time
where the time goes in v6:
time: 51.3 us; the launch traced here: 50.8 us
  Pallas kernels  50.2 us (98%)
  local copies, waits for them, and re-layouts  0.61 us (1%)
    pallas_call x1, Pallas kernels, body(): pl.pallas_call(functools.partial(kernel, lanes, parts), out_shape=pltpu.V...  50.2 us

profile of v6, /device:TPU:80, one launch (start us, length us, event | category | flops | bytes accessed | tf_op | source)
XLA Modules:
  0.0 50.8 jit_solution(16120893916451063384)
XLA Ops:
  0.0 50.2 %hyena_window.1 = bf16[4,4,512]{2,1,0:T(4,128)(2,1)S(1)} custom-call(bf16[4,512,512]{2,1,0:T(8,128)(2,1)} %history.1, bf16[512,512]{1,0:T(8,128)(2,1)} %filter_taps.1, f32[1,512]{1,0:T(1,128)} %bitcast.1, bf16[4,4,512]{2,1,0:T(4,128)(2,1)} %gate_values.1, bf16[192,192]{1,0:T(8,128)(2,1)} %constant.4.clone.ahead_table, bf16[64,192]{1,0:T(8,128)(2,1)} %constant.5.clone.back_table), custom_call_target="tpu_custom_call" | custom-call | tf_op jit(solution)/shard_map/hyena_window/pallas_call | solution.py:506
  50.2 0.6 %copy.8 = bf16[4,4,512]{2,1,0:T(4,128)(2,1)} copy(bf16[4,4,512]{2,1,0:T(4,128)(2,1)S(1)} %hyena_window.1) | data formatting | bytes 32768
